TPU v7x, 8 devices: a whole 2x2x1 slice. The times are simulated.
8 devices in a mesh: batch: 2 (over z, y), row: 4 (over x, core).
Axes of the slice: x: 2, y: 2, z: 1, core: 2. Of those that a mesh axis runs over, the one named last changes fastest.
Arguments:
- trans_mat: bfloat16 [16384, 8192], P(('batch', 'row')), parts along dimension 0
- teleport: float32 [16384, 64], P(('batch', 'row')), parts along dimension 0
- dangling: int32 [16384], P(('batch', 'row')), parts along dimension 0
- damping: float32 [16], replicated
- rank_init: float32 [16384, 64], P(('batch', 'row')), parts along dimension 0
Outputs:
- output: float32 [16384, 64], P(('batch', 'row')), parts along dimension 0
There are 2 independent parts. A program takes and returns all parts, laid end to end along the dimension named above; an argument that names none is the same for every part.
All inputs are finite; a program needn't handle non-finite values.
Results may differ from a plain program's by a relative error of at most 0.001.
Values are sent between devices in bfloat16 or wider.
A program may use at most 1 GiB of HBM per device.

v0:
```python
import jax
import jax.numpy as jnp
from jax import lax
from jax.sharding import PartitionSpec as P, NamedSharding


def solution(mesh):
    spec_rows = P(("batch", "row"), None)
    spec_vec = P(("batch", "row"))

    def local_sweeps(mat_rows, tele_rows, dang_rows, damping, start_rows):
        num_nodes = mat_rows.shape[1]
        dang_float = dang_rows.astype(jnp.float32)
        rank_rows = start_rows
        for sweep_idx in range(damping.shape[0]):
            gathered = lax.all_gather(rank_rows.astype(jnp.bfloat16), "row", axis=0, tiled=True)
            dang_mass = lax.psum(jnp.dot(dang_float, rank_rows, preferred_element_type=jnp.float32), "row")
            prod_rows = jnp.dot(mat_rows, gathered, preferred_element_type=jnp.float32)
            factor = damping[sweep_idx]
            rank_rows = factor * prod_rows + (1.0 - factor) * tele_rows + (factor / num_nodes) * dang_mass[None, :]
        return rank_rows

    sharded_fn = jax.shard_map(local_sweeps, mesh=mesh, in_specs=(spec_rows, spec_rows, spec_vec, P(None), spec_rows), out_specs=spec_rows, check_vma=False)
    return sharded_fn
```

profile of v0, /device:TPU:0, one launch (start us, length us, event | category | flops | bytes accessed | tf_op | source)
XLA Modules:
  0.0 521.2 jit_solution(16063363817143831121)
XLA Ops:
  6.5 1.8 convert_element_type.51
  9.1 1.9 fusion.47
  12.5 1.2 convolution_bitcast_fusion.15
  13.7 9.0 %psum.112 = f32[64]{0:T(128)S(1)} all-reduce(f32[64]{0:T(128)S(1)} %convolution_bitcast_fusion.15), channel_id=1, replica_groups=mesh['batch'=2,'row'=4] {'row'}, use_global_device_ids=true, to_apply=%region_0.0 | all-reduce | flops 64 | bytes 512 | tf_op jit(solution)/shard_map/psum | solution.py:17
  22.7 2.9 all-gather.17.cloned.1.call-done
  25.6 22.6 %fusion.31 = bf16[2048,64]{0,1:T(8,128)(2,1)} fusion(bf16[2048,8192]{1,0:T(8,128)(2,1)} %param.5, bf16[8192,64]{0,1:T(8,128)(2,1)} %all-gather.17.cloned.1.call-done, f32[2048,64]{0,1:T(8,128)} %param.6, f32[64]{0:T(128)S(1)} %broadcast_multiply_fusion.15, f32[]{:T(128)S(6)} %sub.48, f32[]{:T(128)} %bitcast.15), kind=kOutput, calls=%fused_computation.47 | convolution fusion | flops 2148139008 | bytes 35389704 | tf_op jit(solution)/shard_map/dot_general | solution.py:18
  49.5 1.1 convolution_bitcast_fusion.14
  50.6 6.4 %psum.113 = f32[64]{0:T(128)S(1)} all-reduce(f32[64]{0:T(128)S(1)} %convolution_bitcast_fusion.14), channel_id=1, replica_groups=mesh['batch'=2,'row'=4] {'row'}, use_global_device_ids=true, to_apply=%region_1.0 | all-reduce | flops 64 | bytes 512 | tf_op jit(solution)/shard_map/psum | solution.py:17
  57.0 5.1 all-gather.19.cloned.1.call-done
  62.1 17.1 %fusion.32 = bf16[2048,64]{0,1:T(8,128)(2,1)} fusion(bf16[8192,64]{0,1:T(8,128)(2,1)} %all-gather.19.cloned.1.call-done, bf16[2048,8192]{1,0:T(8,128)(2,1)} %param.5, f32[2048,64]{0,1:T(8,128)S(1)} %copy-done, f32[64]{0:T(128)S(1)} %broadcast_multiply_fusion.14, f32[]{:T(128)S(6)} %sub.49, f32[]{:T(128)} %bitcast.14), kind=kOutput, calls=%fused_computation.48 | convolution fusion | flops 2148139008 | bytes 35389704 | tf_op jit(solution)/shard_map/dot_general | solution.py:18
  80.6 1.1 convolution_bitcast_fusion.13
  81.7 6.4 %psum.114 = f32[64]{0:T(128)S(1)} all-reduce(f32[64]{0:T(128)S(1)} %convolution_bitcast_fusion.13), channel_id=1, replica_groups=mesh['batch'=2,'row'=4] {'row'}, use_global_device_ids=true, to_apply=%region_2.0 | all-reduce | flops 64 | bytes 512 | tf_op jit(solution)/shard_map/psum | solution.py:17
  88.1 5.1 all-gather.21.cloned.1.call-done
  93.2 17.1 %fusion.33 = bf16[2048,64]{0,1:T(8,128)(2,1)} fusion(bf16[8192,64]{0,1:T(8,128)(2,1)} %all-gather.21.cloned.1.call-done, bf16[2048,8192]{1,0:T(8,128)(2,1)} %param.5, f32[2048,64]{0,1:T(8,128)S(1)} %copy-done, f32[64]{0:T(128)S(1)} %broadcast_multiply_fusion.13, f32[]{:T(128)S(6)} %sub.50, f32[]{:T(128)} %bitcast.13), kind=kOutput, calls=%fused_computation.49 | convolution fusion | flops 2148139008 | bytes 35389704 | tf_op jit(solution)/shard_map/dot_general | solution.py:18
  111.8 1.1 convolution_bitcast_fusion.12
  112.9 6.6 %psum.115 = f32[64]{0:T(128)S(1)} all-reduce(f32[64]{0:T(128)S(1)} %convolution_bitcast_fusion.12), channel_id=1, replica_groups=mesh['batch'=2,'row'=4] {'row'}, use_global_device_ids=true, to_apply=%region_3.0 | all-reduce | flops 64 | bytes 512 | tf_op jit(solution)/shard_map/psum | solution.py:17
  119.5 4.8 all-gather.23.cloned.1.call-done
  124.3 17.1 %fusion.34 = bf16[2048,64]{0,1:T(8,128)(2,1)} fusion(bf16[8192,64]{0,1:T(8,128)(2,1)} %all-gather.23.cloned.1.call-done, bf16[2048,8192]{1,0:T(8,128)(2,1)} %param.5, f32[2048,64]{0,1:T(8,128)S(1)} %copy-done, f32[64]{0:T(128)S(1)} %broadcast_multiply_fusion.12, f32[]{:T(128)S(6)} %sub.51, f32[]{:T(128)} %bitcast.12), kind=kOutput, calls=%fused_computation.50 | convolution fusion | flops 2148139008 | bytes 35389704 | tf_op jit(solution)/shard_map/dot_general | solution.py:18
  142.7 1.1 convolution_bitcast_fusion.11
  143.8 6.0 %psum.116 = f32[64]{0:T(128)S(1)} all-reduce(f32[64]{0:T(128)S(1)} %convolution_bitcast_fusion.11), channel_id=1, replica_groups=mesh['batch'=2,'row'=4] {'row'}, use_global_device_ids=true, to_apply=%region_4.0 | all-reduce | flops 64 | bytes 512 | tf_op jit(solution)/shard_map/psum | solution.py:17
  149.8 5.7 %all-gather.25.cloned.1.call-done = bf16[8192,64]{0,1:T(8,128)(2,1)} async-done(((bf16[2048,64]{0,1:T(8,128)(2,1)}), bf16[8192,64]{0,1:T(8,128)(2,1)}) %all-gather.25.cloned.1.call-update) | async-done | bytes 1048592 | tf_op jit(solution)/shard_map/all_gather | solution.py:16
  155.6 17.0 %fusion.35 = bf16[2048,64]{0,1:T(8,128)(2,1)} fusion(bf16[8192,64]{0,1:T(8,128)(2,1)} %all-gather.25.cloned.1.call-done, bf16[2048,8192]{1,0:T(8,128)(2,1)} %param.5, f32[2048,64]{0,1:T(8,128)S(1)} %copy-done, f32[64]{0:T(128)S(1)} %broadcast_multiply_fusion.11, f32[]{:T(128)S(6)} %sub.52, f32[]{:T(128)} %bitcast.11), kind=kOutput, calls=%fused_computation.51 | convolution fusion | flops 2148139008 | bytes 35389704 | tf_op jit(solution)/shard_map/dot_general | solution.py:18
  174.0 1.1 convolution_bitcast_fusion.10
  175.2 6.4 %psum.117 = f32[64]{0:T(128)S(1)} all-reduce(f32[64]{0:T(128)S(1)} %convolution_bitcast_fusion.10), channel_id=1, replica_groups=mesh['batch'=2,'row'=4] {'row'}, use_global_device_ids=true, to_apply=%region_5.0 | all-reduce | flops 64 | bytes 512 | tf_op jit(solution)/shard_map/psum | solution.py:17
  181.6 5.0 all-gather.27.cloned.1.call-done
  186.6 17.1 %fusion.36 = bf16[2048,64]{0,1:T(8,128)(2,1)} fusion(bf16[8192,64]{0,1:T(8,128)(2,1)} %all-gather.27.cloned.1.call-done, bf16[2048,8192]{1,0:T(8,128)(2,1)} %param.5, f32[2048,64]{0,1:T(8,128)S(1)} %copy-done, f32[64]{0:T(128)S(1)} %broadcast_multiply_fusion.10, f32[]{:T(128)S(6)} %sub.53, f32[]{:T(128)} %bitcast.10), kind=kOutput, calls=%fused_computation.52 | convolution fusion | flops 2148139008 | bytes 35389704 | tf_op jit(solution)/shard_map/dot_general | solution.py:18
  204.9 1.1 convolution_bitcast_fusion.9
  206.1 6.0 %psum.118 = f32[64]{0:T(128)S(1)} all-reduce(f32[64]{0:T(128)S(1)} %convolution_bitcast_fusion.9), channel_id=1, replica_groups=mesh['batch'=2,'row'=4] {'row'}, use_global_device_ids=true, to_apply=%region_6.0 | all-reduce | flops 64 | bytes 512 | tf_op jit(solution)/shard_map/psum | solution.py:17
  212.1 5.8 %all-gather.29.cloned.1.call-done = bf16[8192,64]{0,1:T(8,128)(2,1)} async-done(((bf16[2048,64]{0,1:T(8,128)(2,1)}), bf16[8192,64]{0,1:T(8,128)(2,1)}) %all-gather.29.cloned.1.call-update) | async-done | bytes 1048592 | tf_op jit(solution)/shard_map/all_gather | solution.py:16
  217.8 17.0 %fusion.37 = bf16[2048,64]{0,1:T(8,128)(2,1)} fusion(bf16[8192,64]{0,1:T(8,128)(2,1)} %all-gather.29.cloned.1.call-done, bf16[2048,8192]{1,0:T(8,128)(2,1)} %param.5, f32[2048,64]{0,1:T(8,128)S(1)} %copy-done, f32[64]{0:T(128)S(1)} %broadcast_multiply_fusion.9, f32[]{:T(128)S(6)} %sub.54, f32[]{:T(128)} %bitcast.9), kind=kOutput, calls=%fused_computation.53 | convolution fusion | flops 2148139008 | bytes 35389704 | tf_op jit(solution)/shard_map/dot_general | solution.py:18
  236.2 1.1 convolution_bitcast_fusion.8
  237.3 6.4 %psum.119 = f32[64]{0:T(128)S(1)} all-reduce(f32[64]{0:T(128)S(1)} %convolution_bitcast_fusion.8), channel_id=1, replica_groups=mesh['batch'=2,'row'=4] {'row'}, use_global_device_ids=true, to_apply=%region_7.0 | all-reduce | flops 64 | bytes 512 | tf_op jit(solution)/shard_map/psum | solution.py:17
  243.7 5.1 all-gather.31.cloned.1.call-done
  248.8 17.1 %fusion.38 = bf16[2048,64]{0,1:T(8,128)(2,1)} fusion(bf16[8192,64]{0,1:T(8,128)(2,1)} %all-gather.31.cloned.1.call-done, bf16[2048,8192]{1,0:T(8,128)(2,1)} %param.5, f32[2048,64]{0,1:T(8,128)S(1)} %copy-done, f32[64]{0:T(128)S(1)} %broadcast_multiply_fusion.8, f32[]{:T(128)S(6)} %sub.55, f32[]{:T(128)} %bitcast.8), kind=kOutput, calls=%fused_computation.54 | convolution fusion | flops 2148139008 | bytes 35389704 | tf_op jit(solution)/shard_map/dot_general | solution.py:18
  267.2 1.1 convolution_bitcast_fusion.7
  268.3 6.4 %psum.120 = f32[64]{0:T(128)S(1)} all-reduce(f32[64]{0:T(128)S(1)} %convolution_bitcast_fusion.7), channel_id=1, replica_groups=mesh['batch'=2,'row'=4] {'row'}, use_global_device_ids=true, to_apply=%region_8.0 | all-reduce | flops 64 | bytes 512 | tf_op jit(solution)/shard_map/psum | solution.py:17
  274.7 5.2 all-gather.33.cloned.1.call-done
  279.9 17.1 %fusion.39 = bf16[2048,64]{0,1:T(8,128)(2,1)} fusion(bf16[8192,64]{0,1:T(8,128)(2,1)} %all-gather.33.cloned.1.call-done, bf16[2048,8192]{1,0:T(8,128)(2,1)} %param.5, f32[2048,64]{0,1:T(8,128)S(1)} %copy-done, f32[64]{0:T(128)S(1)} %broadcast_multiply_fusion.7, f32[]{:T(128)S(6)} %sub.56, f32[]{:T(128)} %bitcast.7), kind=kOutput, calls=%fused_computation.55 | convolution fusion | flops 2148139008 | bytes 35389704 | tf_op jit(solution)/shard_map/dot_general | solution.py:18
  298.3 1.1 convolution_bitcast_fusion.6
  299.4 6.7 %psum.121 = f32[64]{0:T(128)S(1)} all-reduce(f32[64]{0:T(128)S(1)} %convolution_bitcast_fusion.6), channel_id=1, replica_groups=mesh['batch'=2,'row'=4] {'row'}, use_global_device_ids=true, to_apply=%region_9.0 | all-reduce | flops 64 | bytes 512 | tf_op jit(solution)/shard_map/psum | solution.py:17
  306.1 4.9 all-gather.35.cloned.1.call-done
  311.0 17.1 %fusion.40 = bf16[2048,64]{0,1:T(8,128)(2,1)} fusion(bf16[8192,64]{0,1:T(8,128)(2,1)} %all-gather.35.cloned.1.call-done, bf16[2048,8192]{1,0:T(8,128)(2,1)} %param.5, f32[2048,64]{0,1:T(8,128)S(1)} %copy-done, f32[64]{0:T(128)S(1)} %broadcast_multiply_fusion.6, f32[]{:T(128)S(6)} %sub.57, f32[]{:T(128)} %bitcast.6), kind=kOutput, calls=%fused_computation.56 | convolution fusion | flops 2148139008 | bytes 35389704 | tf_op jit(solution)/shard_map/dot_general | solution.py:18
  329.4 1.1 convolution_bitcast_fusion.5
  330.5 6.4 %psum.122 = f32[64]{0:T(128)S(1)} all-reduce(f32[64]{0:T(128)S(1)} %convolution_bitcast_fusion.5), channel_id=1, replica_groups=mesh['batch'=2,'row'=4] {'row'}, use_global_device_ids=true, to_apply=%region_10.0 | all-reduce | flops 64 | bytes 512 | tf_op jit(solution)/shard_map/psum | solution.py:17
  336.9 5.1 all-gather.37.cloned.1.call-done
  342.1 17.1 %fusion.41 = bf16[2048,64]{0,1:T(8,128)(2,1)} fusion(bf16[8192,64]{0,1:T(8,128)(2,1)} %all-gather.37.cloned.1.call-done, bf16[2048,8192]{1,0:T(8,128)(2,1)} %param.5, f32[2048,64]{0,1:T(8,128)S(1)} %copy-done, f32[64]{0:T(128)S(1)} %broadcast_multiply_fusion.5, f32[]{:T(128)S(6)} %sub.58, f32[]{:T(128)} %bitcast.5), kind=kOutput, calls=%fused_computation.57 | convolution fusion | flops 2148139008 | bytes 35389704 | tf_op jit(solution)/shard_map/dot_general | solution.py:18
  360.5 1.1 convolution_bitcast_fusion.4
  361.6 6.4 %psum.123 = f32[64]{0:T(128)S(1)} all-reduce(f32[64]{0:T(128)S(1)} %convolution_bitcast_fusion.4), channel_id=1, replica_groups=mesh['batch'=2,'row'=4] {'row'}, use_global_device_ids=true, to_apply=%region_11.0 | all-reduce | flops 64 | bytes 512 | tf_op jit(solution)/shard_map/psum | solution.py:17
  368.1 5.1 all-gather.39.cloned.1.call-done
  373.1 17.1 %fusion.42 = bf16[2048,64]{0,1:T(8,128)(2,1)} fusion(bf16[8192,64]{0,1:T(8,128)(2,1)} %all-gather.39.cloned.1.call-done, bf16[2048,8192]{1,0:T(8,128)(2,1)} %param.5, f32[2048,64]{0,1:T(8,128)S(1)} %copy-done, f32[64]{0:T(128)S(1)} %broadcast_multiply_fusion.4, f32[]{:T(128)S(6)} %sub.59, f32[]{:T(128)} %bitcast.4), kind=kOutput, calls=%fused_computation.58 | convolution fusion | flops 2148139008 | bytes 35389704 | tf_op jit(solution)/shard_map/dot_general | solution.py:18
  391.5 1.1 convolution_bitcast_fusion.3
  392.7 6.4 %psum.124 = f32[64]{0:T(128)S(1)} all-reduce(f32[64]{0:T(128)S(1)} %convolution_bitcast_fusion.3), channel_id=1, replica_groups=mesh['batch'=2,'row'=4] {'row'}, use_global_device_ids=true, to_apply=%region_12.0 | all-reduce | flops 64 | bytes 512 | tf_op jit(solution)/shard_map/psum | solution.py:17
  399.1 5.1 all-gather.41.cloned.1.call-done
  404.2 17.1 %fusion.43 = bf16[2048,64]{0,1:T(8,128)(2,1)} fusion(bf16[8192,64]{0,1:T(8,128)(2,1)} %all-gather.41.cloned.1.call-done, bf16[2048,8192]{1,0:T(8,128)(2,1)} %param.5, f32[2048,64]{0,1:T(8,128)S(1)} %copy-done, f32[64]{0:T(128)S(1)} %broadcast_multiply_fusion.3, f32[]{:T(128)S(6)} %sub.60, f32[]{:T(128)} %bitcast.3), kind=kOutput, calls=%fused_computation.59 | convolution fusion | flops 2148139008 | bytes 35389704 | tf_op jit(solution)/shard_map/dot_general | solution.py:18
  422.7 1.1 convolution_bitcast_fusion.2
  423.8 6.4 %psum.125 = f32[64]{0:T(128)S(1)} all-reduce(f32[64]{0:T(128)S(1)} %convolution_bitcast_fusion.2), channel_id=1, replica_groups=mesh['batch'=2,'row'=4] {'row'}, use_global_device_ids=true, to_apply=%region_13.0 | all-reduce | flops 64 | bytes 512 | tf_op jit(solution)/shard_map/psum | solution.py:17
  430.3 5.0 all-gather.43.cloned.1.call-done
  435.3 17.1 %fusion.44 = bf16[2048,64]{0,1:T(8,128)(2,1)} fusion(bf16[8192,64]{0,1:T(8,128)(2,1)} %all-gather.43.cloned.1.call-done, bf16[2048,8192]{1,0:T(8,128)(2,1)} %param.5, f32[2048,64]{0,1:T(8,128)S(1)} %copy-done, f32[64]{0:T(128)S(1)} %broadcast_multiply_fusion.2, f32[]{:T(128)S(6)} %sub.61, f32[]{:T(128)} %bitcast.2), kind=kOutput, calls=%fused_computation.60 | convolution fusion | flops 2148139008 | bytes 35389704 | tf_op jit(solution)/shard_map/dot_general | solution.py:18
  454.7 6.0 %psum.126 = f32[64]{0:T(128)S(1)} all-reduce(f32[64]{0:T(128)S(1)} %convolution_bitcast_fusion.1), channel_id=1, replica_groups=mesh['batch'=2,'row'=4] {'row'}, use_global_device_ids=true, to_apply=%region_14.0 | all-reduce | flops 64 | bytes 512 | tf_op jit(solution)/shard_map/psum | solution.py:17
  460.7 5.7 %all-gather.45.cloned.1.call-done = bf16[8192,64]{0,1:T(8,128)(2,1)} async-done(((bf16[2048,64]{0,1:T(8,128)(2,1)}), bf16[8192,64]{0,1:T(8,128)(2,1)}) %all-gather.45.cloned.1.call-update) | async-done | bytes 1048592 | tf_op jit(solution)/shard_map/all_gather | solution.py:16
  466.5 17.0 %fusion.45 = bf16[2048,64]{0,1:T(8,128)(2,1)} fusion(bf16[8192,64]{0,1:T(8,128)(2,1)} %all-gather.45.cloned.1.call-done, bf16[2048,8192]{1,0:T(8,128)(2,1)} %param.5, f32[2048,64]{0,1:T(8,128)S(1)} %copy-done, f32[64]{0:T(128)S(1)} %broadcast_multiply_fusion.1, f32[]{:T(128)S(6)} %sub.62, f32[]{:T(128)} %bitcast.1), kind=kOutput, calls=%fused_computation.61 | convolution fusion | flops 2148139008 | bytes 35389704 | tf_op jit(solution)/shard_map/dot_general | solution.py:18
  485.9 6.4 %psum.127 = f32[64]{0:T(128)S(1)} all-reduce(f32[64]{0:T(128)S(1)} %convolution_bitcast_fusion), channel_id=1, replica_groups=mesh['batch'=2,'row'=4] {'row'}, use_global_device_ids=true, to_apply=%region_15.0 | all-reduce | flops 64 | bytes 512 | tf_op jit(solution)/shard_map/psum | solution.py:17
  492.4 5.2 all-gather.47.cloned.1.call-done
  497.5 17.2 %fusion.46 = f32[2048,64]{0,1:T(8,128)} fusion(bf16[8192,64]{0,1:T(8,128)(2,1)} %all-gather.47.cloned.1.call-done, bf16[2048,8192]{1,0:T(8,128)(2,1)} %param.5, f32[2048,64]{0,1:T(8,128)S(1)} %copy-done, f32[64]{0:T(128)S(1)} %broadcast_multiply_fusion, f32[]{:T(128)S(6)} %sub.63, f32[]{:T(128)} %bitcast), kind=kOutput, calls=%fused_computation.62 | convolution fusion | flops 2148007936 | bytes 35651848 | tf_op jit(solution)/shard_map/dot_general | solution.py:18
  (53 shorter events, 3.9 us)
Async XLA Ops:
  6.5 55.6 %copy-start = (f32[2048,64]{0,1:T(8,128)S(1)}, f32[2048,64]{0,1:T(8,128)}, u32[]{:S(2)}) copy-start(f32[2048,64]{0,1:T(8,128)} %param.6) | copy-start | bytes 1572868
  6.5 19.1 %all-gather.17.cloned.1.call-start = ((), (), s32[]{:S(2)}) async-start(), calls=%async_computation | async-start | bytes 1310720 | tf_op jit(solution)/shard_map/all_gather | solution.py:16
  8.4 53.7 %all-gather.19.cloned.1.call-start = ((), (), s32[]{:S(2)}) async-start(), calls=%async_computation.1 | async-start | bytes 1310720 | tf_op jit(solution)/shard_map/all_gather | solution.py:16
  48.2 45.0 %all-gather.21.cloned.1.call-start = ((), (), s32[]{:S(2)}) async-start(), calls=%async_computation.2 | async-start | bytes 1310720 | tf_op jit(solution)/shard_map/all_gather | solution.py:16
  79.3 45.1 %all-gather.23.cloned.1.call-start = ((), (), s32[]{:S(2)}) async-start(), calls=%async_computation.3 | async-start | bytes 1310720 | tf_op jit(solution)/shard_map/all_gather | solution.py:16
  110.3 45.2 %all-gather.25.cloned.1.call-start = ((), (), s32[]{:S(2)}) async-start(), calls=%async_computation.4 | async-start | bytes 1310720 | tf_op jit(solution)/shard_map/all_gather | solution.py:16
  141.5 45.1 %all-gather.27.cloned.1.call-start = ((), (), s32[]{:S(2)}) async-start(), calls=%async_computation.5 | async-start | bytes 1310720 | tf_op jit(solution)/shard_map/all_gather | solution.py:16
  172.6 45.2 %all-gather.29.cloned.1.call-start = ((), (), s32[]{:S(2)}) async-start(), calls=%async_computation.6 | async-start | bytes 1310720 | tf_op jit(solution)/shard_map/all_gather | solution.py:16
  203.8 45.1 %all-gather.31.cloned.1.call-start = ((), (), s32[]{:S(2)}) async-start(), calls=%async_computation.7 | async-start | bytes 1310720 | tf_op jit(solution)/shard_map/all_gather | solution.py:16
  234.8 45.0 %all-gather.33.cloned.1.call-start = ((), (), s32[]{:S(2)}) async-start(), calls=%async_computation.8 | async-start | bytes 1310720 | tf_op jit(solution)/shard_map/all_gather | solution.py:16
  265.9 45.1 %all-gather.35.cloned.1.call-start = ((), (), s32[]{:S(2)}) async-start(), calls=%async_computation.9 | async-start | bytes 1310720 | tf_op jit(solution)/shard_map/all_gather | solution.py:16
  297.0 45.1 %all-gather.37.cloned.1.call-start = ((), (), s32[]{:S(2)}) async-start(), calls=%async_computation.10 | async-start | bytes 1310720 | tf_op jit(solution)/shard_map/all_gather | solution.py:16
  328.1 45.0 %all-gather.39.cloned.1.call-start = ((), (), s32[]{:S(2)}) async-start(), calls=%async_computation.11 | async-start | bytes 1310720 | tf_op jit(solution)/shard_map/all_gather | solution.py:16
  359.2 45.0 %all-gather.41.cloned.1.call-start = ((), (), s32[]{:S(2)}) async-start(), calls=%async_computation.12 | async-start | bytes 1310720 | tf_op jit(solution)/shard_map/all_gather | solution.py:16
  390.2 45.0 %all-gather.43.cloned.1.call-start = ((), (), s32[]{:S(2)}) async-start(), calls=%async_computation.13 | async-start | bytes 1310720 | tf_op jit(solution)/shard_map/all_gather | solution.py:16
  421.3 45.2 %all-gather.45.cloned.1.call-start = ((), (), s32[]{:S(2)}) async-start(), calls=%async_computation.14 | async-start | bytes 1310720 | tf_op jit(solution)/shard_map/all_gather | solution.py:16
  452.4 45.1 %all-gather.47.cloned.1.call-start = ((), (), s32[]{:S(2)}) async-start(), calls=%async_computation.15 | async-start | bytes 1310720 | tf_op jit(solution)/shard_map/all_gather | solution.py:16
Sparse Core Ops, SparseCore 0:
  8.9 16.6 all-gather.16
  48.3 13.7 all-gather.18
  79.4 13.7 all-gather.20
  110.4 13.8 all-gather.22
  141.6 13.8 all-gather.24
  172.7 13.7 all-gather.26
  203.9 13.8 all-gather.28
  235.0 13.7 all-gather.30
  266.1 13.7 all-gather.32
  297.1 13.8 all-gather.34
  328.2 13.7 all-gather.36
  359.3 13.7 all-gather.38
  390.4 13.7 all-gather.40
  421.4 13.7 all-gather.42
  452.6 13.8 all-gather.44
  483.7 13.7 all-gather.46
where the time goes:
time: 523 us; the launch traced here: 521 us
  matrix products  297 us (57%)
  blocking collectives  105 us (20%)
  waiting for transfers between devices  80.9 us (15%)
  between operations  33.5 us (6%)
    dot_general x16, matrix products, local_sweeps(): prod_rows = jnp.dot(mat_rows, gathered, preferred_element_type=jnp.float32)  279 us
    psum x16, blocking collectives, local_sweeps(): lax.psum(jnp.dot(dang_float, rank_rows, preferred_element_type=jnp.float3...  105 us
    all_gather x16, waiting for transfers between devices, local_sweeps(): lax.all_gather(rank_rows.astype(jnp.bfloat16), 'row', axis=0, tiled=True)  80.7 us
    dot_general x16, matrix products, local_sweeps(): jnp.dot(dang_float, rank_rows, preferred_element_type=jnp.float32)  18 us
  transfers between devices with their start and end apart: 16, of which 16 were waited for; matrix products, arithmetic and copies ran while one was open for 4% of the time, Pallas kernels for 0%

commit v1 on v0

v1 whole, which is shorter than its diff:
```python
import functools

import jax
import jax.numpy as jnp
from jax import lax
from jax.experimental import pallas as pl
from jax.experimental.pallas import tpu as pltpu
from jax.sharding import PartitionSpec as P

MESH = pl.DeviceIdType.MESH
TILE = 256
WIDE = 512
RING = 12
OWN, SIB, CROSS, DIAG = range(4)


def _kernel(sweeps, seeds, nodes, mat_hbm, tele_hbm, dang_ref, damp_ref, init_hbm, out_ref,
            mat_t, stage, ranks, tele_t, init_t, local_sum, mass,
            stage_sem, raw_sem, send_sem, recv_sem, fwd_sem, msend_sem, mrecv_sem):
    part_rows = seeds // 2
    wides = nodes // WIDE
    tiles = nodes // TILE
    batch = lax.axis_index("batch")
    row = lax.axis_index("row")
    chip, core = row // 2, row % 2
    sib, cross, diag = chip * 2 + 1 - core, (1 - chip) * 2 + core, (1 - chip) * 2 + 1 - core
    blocks = (row, sib, cross, diag)

    def own_copy(par, ph, target):
        return pltpu.make_async_remote_copy(
            src_ref=ranks.at[par, OWN, ph], dst_ref=ranks.at[par, target, ph],
            send_sem=send_sem.at[par, ph, target - 1], recv_sem=recv_sem.at[par, ph, target - 1],
            device_id=(batch, blocks[target]), device_id_type=MESH)

    def fwd_copy(par, ph):
        return pltpu.make_async_remote_copy(
            src_ref=ranks.at[par, CROSS, ph], dst_ref=ranks.at[par, DIAG, ph],
            send_sem=fwd_sem.at[par, ph], recv_sem=recv_sem.at[par, ph, DIAG - 1],
            device_id=(batch, sib), device_id_type=MESH)

    def mass_copy(par, ph, target):
        return pltpu.make_async_remote_copy(
            src_ref=mass.at[par, ph, OWN], dst_ref=mass.at[par, ph, target],
            send_sem=msend_sem.at[par, ph, target - 1], recv_sem=mrecv_sem.at[par, ph, target - 1],
            device_id=(batch, blocks[target]), device_id_type=MESH)

    def send(par, ph):
        own_copy(par, ph, CROSS).start()
        own_copy(par, ph, SIB).start()

    def mass_part(val, n, width):
        part = jnp.zeros((val.shape[0], 128), jnp.float32)
        for i in range(width // 128):
            r = n * (width // 128) + i
            part = part + val[:, i * 128:(i + 1) * 128] * dang_ref[r:r + 1, :].astype(jnp.float32)
        return part

    def send_mass(par, ph, part):
        mass[par, ph, OWN, 0:1, 0:part_rows] = jnp.sum(part.T, axis=0, keepdims=True)
        for target in (CROSS, DIAG, SIB):
            mass_copy(par, ph, target).start()

    def get_mass(par, ph):
        for target in (CROSS, DIAG, SIB):
            mass_copy(par, ph, target).wait_recv()
        line = [mass[par, ph, s, 0:1, 0:part_rows] for s in range(4)]
        total = (line[OWN] + line[SIB]) + (line[CROSS] + line[DIAG])
        return jnp.broadcast_to(total, (128, part_rows)).T

    init_copy = pltpu.make_async_copy(init_hbm, init_t, raw_sem.at[0])
    tele_copy = pltpu.make_async_copy(tele_hbm, tele_t, raw_sem.at[1])
    init_copy.start()

    def stage_copy(s, c, buf):
        return pltpu.make_async_copy(
            mat_hbm.at[pl.ds(pl.multiple_of(c * TILE, TILE), TILE), pl.ds(pl.multiple_of(blocks[s] * nodes, nodes), nodes)],
            stage.at[buf], stage_sem.at[buf])

    for i in range(RING):
        stage_copy(i // tiles, i % tiles, i).start()
    tele_copy.start()

    mass[:, :, OWN] = jnp.zeros_like(mass[:, :, OWN])
    barrier = pltpu.get_barrier_semaphore()
    for peer in (sib, cross, diag):
        pl.semaphore_signal(barrier, inc=1, device_id=(batch, peer), device_id_type=MESH)
    pl.semaphore_wait(barrier, 3)

    init_copy.wait()
    for ph in range(2):
        rows = slice(ph * part_rows, (ph + 1) * part_rows)
        part = jnp.zeros((part_rows, 128), jnp.float32)
        for n in range(wides):
            val = init_t[rows, n * WIDE:(n + 1) * WIDE]
            ranks[0, OWN, ph, :, n * WIDE:(n + 1) * WIDE] = val.astype(jnp.bfloat16)
            part = part + mass_part(val, n, WIDE)
        send(0, ph)
        send_mass(0, ph, part)
    tele_copy.wait()

    total = 4 * tiles

    for s in range(4):
        def load_rows(c, carry, s=s):
            i = s * tiles + c
            buf = lax.rem(i, RING)
            stage_copy(s, c, buf).wait()
            for u in range(2):
                @pl.when(lax.rem(c, 2) == u)
                def _(u=u):
                    for k in range(tiles):
                        mat_t[s, c // 2, k * TILE:(k + 1) * TILE, u * TILE:(u + 1) * TILE] = stage[buf, :, k * TILE:(k + 1) * TILE].T
            for s2 in range(s, 4):
                @pl.when(jnp.logical_and(i + RING >= s2 * tiles, i + RING < (s2 + 1) * tiles))
                def _(s2=s2):
                    stage_copy(s2, i + RING - s2 * tiles, buf).start()
            return carry

        lax.fori_loop(0, tiles, load_rows, 0)

    def lhs(par, s, ph):
        val = ranks[par, s, ph]
        return jnp.concatenate([val] * 4, axis=0)

    def dot(left, s, n):
        return jnp.dot(left, mat_t[s, n], preferred_element_type=jnp.float32)

    def local_pass(par):
        left = jnp.concatenate([ranks[par, OWN, 0], ranks[par, OWN, 1]] * 2, axis=0)
        for n in range(wides):
            local_sum[:, n * WIDE:(n + 1) * WIDE] = dot(left, OWN, n)[:seeds]
        for ph in range(2):
            own_copy(par, ph, SIB).wait_recv()
        left = jnp.concatenate([ranks[par, SIB, 0], ranks[par, SIB, 1]] * 2, axis=0)
        for n in range(wides):
            cols = slice(n * WIDE, (n + 1) * WIDE)
            local_sum[:, cols] = local_sum[:, cols] + dot(left, SIB, n)[:seeds]

    def remote_pass(par, ph, t, store):
        rows = slice(ph * part_rows, (ph + 1) * part_rows)
        own_copy(par, ph, CROSS).wait_recv()
        fwd_copy(par, ph).start()
        left = lhs(par, CROSS, ph)
        for n in range(wides):
            cols = slice(n * WIDE, (n + 1) * WIDE)
            local_sum[rows, cols] = local_sum[rows, cols] + dot(left, CROSS, n)[:part_rows]
        fwd_copy(par, ph).wait_recv()
        msum = get_mass(par, ph)
        factor = damp_ref[t]
        add = (factor * (1.0 / (4 * nodes))) * msum
        add = jnp.concatenate([add] * (WIDE // 128), axis=1)
        left = lhs(par, DIAG, ph)
        for n in range(wides):
            cols = slice(n * WIDE, (n + 1) * WIDE)
            total = local_sum[rows, cols] + dot(left, DIAG, n)[:part_rows]
            store(n, factor * total + (1.0 - factor) * tele_t[rows, cols] + add)

    def done(par, ph):
        own_copy(par, ph, SIB).wait_send()
        own_copy(par, ph, CROSS).wait_send()
        fwd_copy(par, ph).wait_send()
        for target in (CROSS, DIAG, SIB):
            mass_copy(par, ph, target).wait_send()

    def sweep(t, carry):
        par = lax.rem(t, 2)
        nxt = 1 - par
        local_pass(par)
        for ph in range(2):
            parts = []

            def store(n, val, ph=ph, parts=parts):
                ranks[nxt, OWN, ph, :, n * WIDE:(n + 1) * WIDE] = val.astype(jnp.bfloat16)
                parts.append(mass_part(val, n, WIDE))

            remote_pass(par, ph, t, store)
            done(par, ph)
            send(nxt, ph)
            send_mass(nxt, ph, functools.reduce(jnp.add, parts))
        return carry

    lax.fori_loop(0, sweeps - 1, sweep, 0)
    last = sweeps - 1
    par = last % 2
    local_pass(par)
    for ph in range(2):
        def store(n, val, ph=ph):
            out_ref[ph * part_rows:(ph + 1) * part_rows, n * WIDE:(n + 1) * WIDE] = val

        remote_pass(par, ph, last, store)
        done(par, ph)


def solution(mesh):
    spec_rows = P(("batch", "row"), None)
    spec_vec = P(("batch", "row"))

    def local_sweeps(mat_rows, tele_rows, dang_rows, damping, start_rows):
        nodes, seeds = start_rows.shape
        sweeps = damping.shape[0]
        hbm = pl.BlockSpec(memory_space=pl.ANY)
        vmem = pl.BlockSpec(memory_space=pltpu.VMEM)
        dma = pltpu.SemaphoreType.DMA
        out = pl.pallas_call(
            functools.partial(_kernel, sweeps, seeds, nodes),
            out_shape=jax.ShapeDtypeStruct((seeds, nodes), jnp.float32),
            in_specs=[hbm, hbm, vmem, pl.BlockSpec(memory_space=pltpu.SMEM), hbm],
            out_specs=vmem,
            scratch_shapes=[
                pltpu.VMEM((4, nodes // WIDE, nodes, WIDE), jnp.bfloat16),
                pltpu.VMEM((RING, TILE, nodes), jnp.bfloat16),
                pltpu.VMEM((2, 4, 2, seeds // 2, nodes), jnp.bfloat16),
                pltpu.VMEM((seeds, nodes), jnp.float32),
                pltpu.VMEM((seeds, nodes), jnp.float32),
                pltpu.VMEM((seeds, nodes), jnp.float32),
                pltpu.VMEM((2, 2, 4, 8, 128), jnp.float32),
                dma((RING,)), dma((2,)), dma((2, 2, 2)), dma((2, 2, 3)), dma((2, 2)), dma((2, 2, 3)), dma((2, 2, 3)),
            ],
            compiler_params=pltpu.CompilerParams(collective_id=0, has_side_effects=True, vmem_limit_bytes=63 * 2**20),
        )(mat_rows, tele_rows.T, dang_rows.reshape(-1, 128), damping, start_rows.T)
        return out.T

    return jax.shard_map(local_sweeps, mesh=mesh, in_specs=(spec_rows, spec_rows, spec_vec, P(None), spec_rows), out_specs=spec_rows, check_vma=False)
```

time: 523 us -> 148 us (0.28)
  matrix products: 297 us -> 0 us
  Pallas kernels: 0 us -> 146 us
  blocking collectives: 105 us -> 0 us
  waiting for transfers between devices: 80.9 us -> 0 us
  between operations: 33.5 us -> 0.01 us
    dot_general x32 -> x0, matrix products: 297 us -> none  [the longest x16 279 us: local_sweeps(): prod_rows = jnp.dot(mat_rows, gathered, preferred_element_type=jnp.float32)]
    pallas_call x0 -> x1, Pallas kernels: none -> 146 us  [local_sweeps(): pl.pallas_call(functools.partial(_kernel, sweeps, seeds, nodes), out_shap...]
    psum x16 -> x0, blocking collectives: 105 us -> none  [local_sweeps(): lax.psum(jnp.dot(dang_float, rank_rows, preferred_element_type=jnp.float3...]
    all_gather x16 -> x0, waiting for transfers between devices: 80.7 us -> none  [local_sweeps(): lax.all_gather(rank_rows.astype(jnp.bfloat16), 'row', axis=0, tiled=True)]
  transfers between devices with their start and end apart: 16 -> 0, of which waited for: 16 -> 0; matrix products, arithmetic and copies ran while one was open for 4% -> 0% of each run, Pallas kernels for 0% -> 0%
where the time goes in v1:
time: 148 us
  Pallas kernels  146 us (99%)
  local copies, waits for them, and re-layouts  1.87 us (1%)
    pallas_call x1, Pallas kernels, local_sweeps(): pl.pallas_call(functools.partial(_kernel, sweeps, seeds, nodes), out_shap...  146 us

profile of v1, /device:TPU:0, one launch (start us, length us, event | category | flops | bytes accessed | tf_op | source)
XLA Modules:
  0.0 148.3 jit_solution(15850506661617439042)
XLA Ops:
  0.0 146.4 %shard_map.55 = f32[64,2048]{1,0:T(8,128)} custom-call(bf16[2048,8192]{1,0:T(8,128)(2,1)} %mat_hbm.1, f32[64,2048]{1,0:T(8,128)} %bitcast.5, s32[16,128]{1,0:T(8,128)} %bitcast.7, f32[16]{0:T(128)} %damp_ref.1, f32[64,2048]{1,0:T(8,128)} %bitcast.6), custom_call_target="tpu_custom_call" | custom-call | tf_op jit(solution)/shard_map/pallas_call | solution.py:204
  146.4 1.9 %copy.7 = f32[2048,64]{0,1:T(8,128)} copy(f32[2048,64]{0,1:T(8,128)} %bitcast.4) | data formatting | bytes 1048576

commit v2 on v1

--- a/solution.py
+++ b/solution.py
@@ -10,7 +10,8 @@
 MESH = pl.DeviceIdType.MESH
 TILE = 256
 WIDE = 512
-RING = 12
+RING = 6
+CROSS_AT = 11
 OWN, SIB, CROSS, DIAG = range(4)
 
 
@@ -71,13 +72,15 @@
     tele_copy = pltpu.make_async_copy(tele_hbm, tele_t, raw_sem.at[1])
     init_copy.start()
 
-    def stage_copy(s, c, buf):
+    def stage_copy(i):
+        s, n = i // wides, i % wides
+        block = ((chip + s // 2) % 2) * 2 + (core + s % 2) % 2
         return pltpu.make_async_copy(
-            mat_hbm.at[pl.ds(pl.multiple_of(c * TILE, TILE), TILE), pl.ds(pl.multiple_of(blocks[s] * nodes, nodes), nodes)],
-            stage.at[buf], stage_sem.at[buf])
+            mat_hbm.at[pl.ds(pl.multiple_of(n * WIDE, WIDE), WIDE), pl.ds(pl.multiple_of(block * nodes, nodes), nodes)],
+            stage.at[i % RING], stage_sem.at[i % RING])
 
     for i in range(RING):
-        stage_copy(i // tiles, i % tiles, i).start()
+        stage_copy(i).start()
     tele_copy.start()
 
     mass[:, :, OWN] = jnp.zeros_like(mass[:, :, OWN])
@@ -98,25 +101,8 @@
         send_mass(0, ph, part)
     tele_copy.wait()
 
-    total = 4 * tiles
-
-    for s in range(4):
-        def load_rows(c, carry, s=s):
-            i = s * tiles + c
-            buf = lax.rem(i, RING)
-            stage_copy(s, c, buf).wait()
-            for u in range(2):
-                @pl.when(lax.rem(c, 2) == u)
-                def _(u=u):
-                    for k in range(tiles):
-                        mat_t[s, c // 2, k * TILE:(k + 1) * TILE, u * TILE:(u + 1) * TILE] = stage[buf, :, k * TILE:(k + 1) * TILE].T
-            for s2 in range(s, 4):
-                @pl.when(jnp.logical_and(i + RING >= s2 * tiles, i + RING < (s2 + 1) * tiles))
-                def _(s2=s2):
-                    stage_copy(s2, i + RING - s2 * tiles, buf).start()
-            return carry
-
-        lax.fori_loop(0, tiles, load_rows, 0)
+    def cols_of(n):
+        return slice(n * WIDE, (n + 1) * WIDE)
 
     def lhs(par, s, ph):
         val = ranks[par, s, ph]
@@ -162,6 +148,55 @@
         for target in (CROSS, DIAG, SIB):
             mass_copy(par, ph, target).wait_send()
 
+    def load_piece(i):
+        stage_copy(i).wait()
+        for k in range(tiles):
+            for u in range(WIDE // TILE):
+                mat_t[i // wides, i % wides, k * TILE:(k + 1) * TILE, u * TILE:(u + 1) * TILE] = (
+                    stage[i % RING, u * TILE:(u + 1) * TILE, k * TILE:(k + 1) * TILE].T)
+
+        if i + RING < 4 * wides:
+            stage_copy(i + RING).start()
+
+    def both(par, s):
+        return jnp.concatenate([ranks[par, s, 0], ranks[par, s, 1]] * 2, axis=0)
+
+    def first_dot(s, n):
+        prod = dot(both(0, s), s, n)[:seeds]
+        local_sum[:, cols_of(n)] = prod if s == OWN else local_sum[:, cols_of(n)] + prod
+
+    for i in range(4 * wides):
+        if i == wides + 1:
+            for ph in range(2):
+                own_copy(0, ph, SIB).wait_recv()
+        if i == CROSS_AT:
+            for ph in range(2):
+                own_copy(0, ph, CROSS).wait_recv()
+                fwd_copy(0, ph).start()
+        load_piece(i)
+        if 1 <= i <= 2 * wides:
+            first_dot((i - 1) // wides, (i - 1) % wides)
+        if i >= 3 * wides:
+            first_dot(CROSS, i - 3 * wides)
+    first_parts = []
+    for ph in range(2):
+        fwd_copy(0, ph).wait_recv()
+    sums = [get_mass(0, ph) for ph in range(2)]
+    add = (damp_ref[0] * (1.0 / (4 * nodes))) * jnp.concatenate(sums, axis=0)
+    add = jnp.concatenate([add] * (WIDE // 128), axis=1)
+    for n in range(wides):
+        total = local_sum[:, cols_of(n)] + dot(both(0, DIAG), DIAG, n)[:seeds]
+        val = damp_ref[0] * total + (1.0 - damp_ref[0]) * tele_t[:, cols_of(n)] + add
+        for ph in range(2):
+            ranks[1, OWN, ph, :, cols_of(n)] = val[ph * part_rows:(ph + 1) * part_rows].astype(jnp.bfloat16)
+        first_parts.append(mass_part(val, n, WIDE))
+    first_part = functools.reduce(jnp.add, first_parts)
+    for ph in range(2):
+        done(0, ph)
+    for ph in range(2):
+        send(1, ph)
+        send_mass(1, ph, first_part[ph * part_rows:(ph + 1) * part_rows])
+
     def sweep(t, carry):
         par = lax.rem(t, 2)
         nxt = 1 - par
@@ -179,7 +214,7 @@
             send_mass(nxt, ph, functools.reduce(jnp.add, parts))
         return carry
 
-    lax.fori_loop(0, sweeps - 1, sweep, 0)
+    lax.fori_loop(1, sweeps - 1, sweep, 0)
     last = sweeps - 1
     par = last % 2
     local_pass(par)
@@ -208,7 +243,7 @@
             out_specs=vmem,
             scratch_shapes=[
                 pltpu.VMEM((4, nodes // WIDE, nodes, WIDE), jnp.bfloat16),
-                pltpu.VMEM((RING, TILE, nodes), jnp.bfloat16),
+                pltpu.VMEM((RING, WIDE, nodes), jnp.bfloat16),
                 pltpu.VMEM((2, 4, 2, seeds // 2, nodes), jnp.bfloat16),
                 pltpu.VMEM((seeds, nodes), jnp.float32),
                 pltpu.VMEM((seeds, nodes), jnp.float32),

time: 148 us -> 144 us (0.973)
  Pallas kernels: 146 us -> 142 us
    pallas_call x1, Pallas kernels: 146 us -> 142 us  [local_sweeps(): pl.pallas_call(functools.partial(_kernel, sweeps, seeds, nodes), out_shap...]
where the time goes in v2:
time: 144 us; the launch traced here: 143 us
  Pallas kernels  142 us (99%)
  local copies, waits for them, and re-layouts  1.87 us (1%)
    pallas_call x1, Pallas kernels, local_sweeps(): pl.pallas_call(functools.partial(_kernel, sweeps, seeds, nodes), out_shap...  142 us

profile of v2, /device:TPU:0, one launch (start us, length us, event | category | flops | bytes accessed | tf_op | source)
XLA Modules:
  0.0 143.5 jit_solution(6241561597958047017)
XLA Ops:
  0.0 141.6 %shard_map.55 = f32[64,2048]{1,0:T(8,128)} custom-call(bf16[2048,8192]{1,0:T(8,128)(2,1)} %mat_hbm.1, f32[64,2048]{1,0:T(8,128)} %bitcast.5, s32[16,128]{1,0:T(8,128)} %bitcast.7, f32[16]{0:T(128)} %damp_ref.1, f32[64,2048]{1,0:T(8,128)} %bitcast.6), custom_call_target="tpu_custom_call" | custom-call | tf_op jit(solution)/shard_map/pallas_call | solution.py:239
  141.6 1.9 %copy.7 = f32[2048,64]{0,1:T(8,128)} copy(f32[2048,64]{0,1:T(8,128)} %bitcast.4) | data formatting | bytes 1048576

commit v3 on v2

--- a/solution.py
+++ b/solution.py
@@ -12,12 +12,13 @@
 WIDE = 512
 RING = 6
 CROSS_AT = 11
+LATER = {12: ((2, 0), (2, 1)), 13: ((2, 2), (2, 3)), 14: ((3, 0), (3, 1)), 15: ((3, 2),)}
 OWN, SIB, CROSS, DIAG = range(4)
 
 
 def _kernel(sweeps, seeds, nodes, mat_hbm, tele_hbm, dang_ref, damp_ref, init_hbm, out_ref,
             mat_t, stage, ranks, tele_t, init_t, local_sum, mass,
-            stage_sem, raw_sem, send_sem, recv_sem, fwd_sem, msend_sem, mrecv_sem):
+            stage_sem, raw_sem, send_sem, recv_sem, msend_sem, mrecv_sem):
     part_rows = seeds // 2
     wides = nodes // WIDE
     tiles = nodes // TILE
@@ -30,20 +31,26 @@
     def own_copy(par, ph, target):
         return pltpu.make_async_remote_copy(
             src_ref=ranks.at[par, OWN, ph], dst_ref=ranks.at[par, target, ph],
-            send_sem=send_sem.at[par, ph, target - 1], recv_sem=recv_sem.at[par, ph, target - 1],
+            send_sem=send_sem.at[par, ph], recv_sem=recv_sem.at[par, ph, target - 1],
             device_id=(batch, blocks[target]), device_id_type=MESH)
 
     def fwd_copy(par, ph):
         return pltpu.make_async_remote_copy(
             src_ref=ranks.at[par, CROSS, ph], dst_ref=ranks.at[par, DIAG, ph],
-            send_sem=fwd_sem.at[par, ph], recv_sem=recv_sem.at[par, ph, DIAG - 1],
+            send_sem=send_sem.at[par, ph], recv_sem=recv_sem.at[par, ph, DIAG - 1],
             device_id=(batch, sib), device_id_type=MESH)
 
     def mass_copy(par, ph, target):
         return pltpu.make_async_remote_copy(
             src_ref=mass.at[par, ph, OWN], dst_ref=mass.at[par, ph, target],
-            send_sem=msend_sem.at[par, ph, target - 1], recv_sem=mrecv_sem.at[par, ph, target - 1],
+            send_sem=msend_sem.at[par, ph], recv_sem=mrecv_sem.at[par, ph],
             device_id=(batch, blocks[target]), device_id_type=MESH)
+
+    def mass_all(par, ph):
+        return pltpu.make_async_remote_copy(
+            src_ref=mass.at[par, ph, 1:4], dst_ref=mass.at[par, ph, 1:4],
+            send_sem=msend_sem.at[par, ph], recv_sem=mrecv_sem.at[par, ph],
+            device_id=(batch, sib), device_id_type=MESH)
 
     def send(par, ph):
         own_copy(par, ph, CROSS).start()
@@ -62,8 +69,7 @@
             mass_copy(par, ph, target).start()
 
     def get_mass(par, ph):
-        for target in (CROSS, DIAG, SIB):
-            mass_copy(par, ph, target).wait_recv()
+        mass_all(par, ph).wait_recv()
         line = [mass[par, ph, s, 0:1, 0:part_rows] for s in range(4)]
         total = (line[OWN] + line[SIB]) + (line[CROSS] + line[DIAG])
         return jnp.broadcast_to(total, (128, part_rows)).T
@@ -142,11 +148,11 @@
             store(n, factor * total + (1.0 - factor) * tele_t[rows, cols] + add)
 
     def done(par, ph):
-        own_copy(par, ph, SIB).wait_send()
-        own_copy(par, ph, CROSS).wait_send()
-        fwd_copy(par, ph).wait_send()
-        for target in (CROSS, DIAG, SIB):
-            mass_copy(par, ph, target).wait_send()
+        pltpu.make_async_remote_copy(
+            src_ref=ranks.at[par, 0:3, ph], dst_ref=ranks.at[par, 0:3, ph],
+            send_sem=send_sem.at[par, ph], recv_sem=recv_sem.at[par, ph, 0],
+            device_id=(batch, sib), device_id_type=MESH).wait_send()
+        mass_all(par, ph).wait_send()
 
     def load_piece(i):
         stage_copy(i).wait()
@@ -176,16 +182,19 @@
         load_piece(i)
         if 1 <= i <= 2 * wides:
             first_dot((i - 1) // wides, (i - 1) % wides)
-        if i >= 3 * wides:
-            first_dot(CROSS, i - 3 * wides)
+        if i == 4 * wides - 2:
+            for ph in range(2):
+                fwd_copy(0, ph).wait_recv()
+        for s, n in LATER.get(i, ()):
+            first_dot(s, n)
     first_parts = []
-    for ph in range(2):
-        fwd_copy(0, ph).wait_recv()
     sums = [get_mass(0, ph) for ph in range(2)]
     add = (damp_ref[0] * (1.0 / (4 * nodes))) * jnp.concatenate(sums, axis=0)
     add = jnp.concatenate([add] * (WIDE // 128), axis=1)
     for n in range(wides):
-        total = local_sum[:, cols_of(n)] + dot(both(0, DIAG), DIAG, n)[:seeds]
+        total = local_sum[:, cols_of(n)]
+        if n == wides - 1:
+            total = total + dot(both(0, DIAG), DIAG, n)[:seeds]
         val = damp_ref[0] * total + (1.0 - damp_ref[0]) * tele_t[:, cols_of(n)] + add
         for ph in range(2):
             ranks[1, OWN, ph, :, cols_of(n)] = val[ph * part_rows:(ph + 1) * part_rows].astype(jnp.bfloat16)
@@ -249,9 +258,9 @@
                 pltpu.VMEM((seeds, nodes), jnp.float32),
                 pltpu.VMEM((seeds, nodes), jnp.float32),
                 pltpu.VMEM((2, 2, 4, 8, 128), jnp.float32),
-                dma((RING,)), dma((2,)), dma((2, 2, 2)), dma((2, 2, 3)), dma((2, 2)), dma((2, 2, 3)), dma((2, 2, 3)),
+                dma((RING,)), dma((2,)), dma((2, 2)), dma((2, 2, 3)), dma((2, 2)), dma((2, 2)),
             ],
-            compiler_params=pltpu.CompilerParams(collective_id=0, has_side_effects=True, vmem_limit_bytes=63 * 2**20),
+            compiler_params=pltpu.CompilerParams(collective_id=0, has_side_effects=True, vmem_limit_bytes=50 * 2**20),
         )(mat_rows, tele_rows.T, dang_rows.reshape(-1, 128), damping, start_rows.T)
         return out.T
 

time: 144 us -> 142 us (0.986)
  Pallas kernels: 142 us -> 137 us
  local copies, waits for them, and re-layouts: 1.87 us -> 4.23 us
    pallas_call x1, Pallas kernels: 142 us -> 137 us  [local_sweeps(): pl.pallas_call(functools.partial(_kernel, sweeps, seeds, nodes), out_shap...]
    unnamed x1 -> x9, local copies, waits for them, and re-layouts: 1.87 us -> 4.23 us
where the time goes in v3:
time: 142 us; the launch traced here: 141 us
  Pallas kernels  137 us (96%)
  local copies, waits for them, and re-layouts  4.23 us (3%)
    pallas_call x1, Pallas kernels, local_sweeps(): pl.pallas_call(functools.partial(_kernel, sweeps, seeds, nodes), out_shap...  137 us
    unnamed x9, local copies, waits for them, and re-layouts  4.23 us

profile of v3, /device:TPU:0, one launch (start us, length us, event | category | flops | bytes accessed | tf_op | source)
XLA Modules:
  0.0 141.5 jit_solution(14045522309767572769)
XLA Ops:
  0.0 0.0 copy-start
  0.0 1.0 copy-done
  1.0 0.0 copy-start.1
  1.0 1.0 copy-done.1
  2.1 0.0 copy-start.2
  2.1 0.7 copy-done.2
  2.8 0.0 copy-start.3
  2.8 0.7 copy-done.3
  3.4 137.2 %shard_map.55 = f32[64,2048]{1,0:T(8,128)S(1)} custom-call(bf16[2048,8192]{1,0:T(8,128)(2,1)} %mat_hbm.1, f32[64,2048]{1,0:T(8,128)S(1)} %bitcast.5, s32[16,128]{1,0:T(8,128)S(1)} %bitcast.7, f32[16]{0:T(128)S(1)} %copy-done.3, f32[64,2048]{1,0:T(8,128)S(1)} %bitcast.6), custom_call_target="tpu_custom_call" | custom-call | tf_op jit(solution)/shard_map/pallas_call | solution.py:248
  140.7 0.8 copy.7
Async XLA Ops:
  0.0 1.0 copy-start
  1.0 1.0 copy-start.1
  2.1 0.7 copy-start.2
  2.8 0.7 copy-start.3

commit v4 on v3

--- a/solution.py
+++ b/solution.py
@@ -16,9 +16,9 @@
 OWN, SIB, CROSS, DIAG = range(4)
 
 
-def _kernel(sweeps, seeds, nodes, mat_hbm, tele_hbm, dang_ref, damp_ref, init_hbm, out_ref,
-            mat_t, stage, ranks, tele_t, init_t, local_sum, mass,
-            stage_sem, raw_sem, send_sem, recv_sem, msend_sem, mrecv_sem):
+def _kernel(sweeps, seeds, nodes, mat_hbm, tele_ref, dang_ref, damp_ref, init_ref, out_ref,
+            mat_t, stage, ranks, local_sum, mass,
+            stage_sem, send_sem, recv_sem, msend_sem, mrecv_sem):
     part_rows = seeds // 2
     wides = nodes // WIDE
     tiles = nodes // TILE
@@ -74,10 +74,6 @@
         total = (line[OWN] + line[SIB]) + (line[CROSS] + line[DIAG])
         return jnp.broadcast_to(total, (128, part_rows)).T
 
-    init_copy = pltpu.make_async_copy(init_hbm, init_t, raw_sem.at[0])
-    tele_copy = pltpu.make_async_copy(tele_hbm, tele_t, raw_sem.at[1])
-    init_copy.start()
-
     def stage_copy(i):
         s, n = i // wides, i % wides
         block = ((chip + s // 2) % 2) * 2 + (core + s % 2) % 2
@@ -87,7 +83,6 @@
 
     for i in range(RING):
         stage_copy(i).start()
-    tele_copy.start()
 
     mass[:, :, OWN] = jnp.zeros_like(mass[:, :, OWN])
     barrier = pltpu.get_barrier_semaphore()
@@ -95,17 +90,15 @@
         pl.semaphore_signal(barrier, inc=1, device_id=(batch, peer), device_id_type=MESH)
     pl.semaphore_wait(barrier, 3)
 
-    init_copy.wait()
     for ph in range(2):
         rows = slice(ph * part_rows, (ph + 1) * part_rows)
         part = jnp.zeros((part_rows, 128), jnp.float32)
         for n in range(wides):
-            val = init_t[rows, n * WIDE:(n + 1) * WIDE]
+            val = init_ref[rows, n * WIDE:(n + 1) * WIDE]
             ranks[0, OWN, ph, :, n * WIDE:(n + 1) * WIDE] = val.astype(jnp.bfloat16)
             part = part + mass_part(val, n, WIDE)
         send(0, ph)
         send_mass(0, ph, part)
-    tele_copy.wait()
 
     def cols_of(n):
         return slice(n * WIDE, (n + 1) * WIDE)
@@ -145,7 +138,7 @@
         for n in range(wides):
             cols = slice(n * WIDE, (n + 1) * WIDE)
             total = local_sum[rows, cols] + dot(left, DIAG, n)[:part_rows]
-            store(n, factor * total + (1.0 - factor) * tele_t[rows, cols] + add)
+            store(n, factor * total + (1.0 - factor) * tele_ref[rows, cols] + add)
 
     def done(par, ph):
         pltpu.make_async_remote_copy(
@@ -195,7 +188,7 @@
         total = local_sum[:, cols_of(n)]
         if n == wides - 1:
             total = total + dot(both(0, DIAG), DIAG, n)[:seeds]
-        val = damp_ref[0] * total + (1.0 - damp_ref[0]) * tele_t[:, cols_of(n)] + add
+        val = damp_ref[0] * total + (1.0 - damp_ref[0]) * tele_ref[:, cols_of(n)] + add
         for ph in range(2):
             ranks[1, OWN, ph, :, cols_of(n)] = val[ph * part_rows:(ph + 1) * part_rows].astype(jnp.bfloat16)
         first_parts.append(mass_part(val, n, WIDE))
@@ -248,17 +241,15 @@
         out = pl.pallas_call(
             functools.partial(_kernel, sweeps, seeds, nodes),
             out_shape=jax.ShapeDtypeStruct((seeds, nodes), jnp.float32),
-            in_specs=[hbm, hbm, vmem, pl.BlockSpec(memory_space=pltpu.SMEM), hbm],
+            in_specs=[hbm, vmem, vmem, pl.BlockSpec(memory_space=pltpu.SMEM), vmem],
             out_specs=vmem,
             scratch_shapes=[
                 pltpu.VMEM((4, nodes // WIDE, nodes, WIDE), jnp.bfloat16),
                 pltpu.VMEM((RING, WIDE, nodes), jnp.bfloat16),
                 pltpu.VMEM((2, 4, 2, seeds // 2, nodes), jnp.bfloat16),
                 pltpu.VMEM((seeds, nodes), jnp.float32),
-                pltpu.VMEM((seeds, nodes), jnp.float32),
-                pltpu.VMEM((seeds, nodes), jnp.float32),
                 pltpu.VMEM((2, 2, 4, 8, 128), jnp.float32),
-                dma((RING,)), dma((2,)), dma((2, 2)), dma((2, 2, 3)), dma((2, 2)), dma((2, 2)),
+                dma((RING,)), dma((2, 2)), dma((2, 2, 3)), dma((2, 2)), dma((2, 2)),
             ],
             compiler_params=pltpu.CompilerParams(collective_id=0, has_side_effects=True, vmem_limit_bytes=50 * 2**20),
         )(mat_rows, tele_rows.T, dang_rows.reshape(-1, 128), damping, start_rows.T)

time: 142 us -> 142 us (level)
  no operation moved by 1% of the time
where the time goes in v4:
time: 142 us; the launch traced here: 141 us
  Pallas kernels  137 us (96%)
  local copies, waits for them, and re-layouts  4.23 us (3%)
    pallas_call x1, Pallas kernels, local_sweeps(): pl.pallas_call(functools.partial(_kernel, sweeps, seeds, nodes), out_shap...  137 us
    unnamed x9, local copies, waits for them, and re-layouts  4.23 us

profile of v4, /device:TPU:0, one launch (start us, length us, event | category | flops | bytes accessed | tf_op | source)
XLA Modules:
  0.0 141.4 jit_solution(11161048790395570155)
XLA Ops:
  0.0 0.0 copy-start
  0.0 1.0 copy-done
  1.0 0.0 copy-start.1
  1.0 1.0 copy-done.1
  2.1 0.0 copy-start.2
  2.1 0.7 copy-done.2
  2.8 0.0 copy-start.3
  2.8 0.7 copy-done.3
  3.4 137.2 %shard_map.55 = f32[64,2048]{1,0:T(8,128)S(1)} custom-call(bf16[2048,8192]{1,0:T(8,128)(2,1)} %mat_hbm.1, f32[64,2048]{1,0:T(8,128)S(1)} %bitcast.5, s32[16,128]{1,0:T(8,128)S(1)} %bitcast.7, f32[16]{0:T(128)S(1)} %copy-done.3, f32[64,2048]{1,0:T(8,128)S(1)} %bitcast.6), custom_call_target="tpu_custom_call" | custom-call | tf_op jit(solution)/shard_map/pallas_call | solution.py:241
  140.6 0.8 copy.7
Async XLA Ops:
  0.0 1.0 copy-start
  1.0 1.0 copy-start.1
  2.1 0.7 copy-start.2
  2.8 0.7 copy-start.3
